TPU v7x, 256 devices: a whole 4x4x8 slice. The times are simulated.
256 devices in a mesh: visit: 8 (over z), bulk: 32 (over x, y, core).
Axes of the slice: x: 4, y: 4, z: 8, core: 2. Of those that a mesh axis runs over, the one named last changes fastest.
Arguments:
- piece_flux: float32 [8, 32, 32, 128, 128], P('visit', 'bulk'), may hold values from -6 to 6
- piece_ivar: float32 [8, 32, 32, 128, 128], P('visit', 'bulk'), may hold values from 0.5 to 8
- warp_rows: float32 [8, 32, 32, 128, 128], P('visit', 'bulk'), may hold values from 0 to 1, as said below
- warp_cols: float32 [8, 32, 32, 128, 128], P('visit', 'bulk'), may hold values from 0 to 1, as said below
- piece_owner: int32 [8, 32, 32, 1], P('visit', 'bulk'), may hold values from 0 to 31; in each aligned block of 32 rows (0 to 31, 32 to 63, ..., all dimensions but the last counted through in order) at most 2 rows name the same one
- piece_slot: int32 [8, 32, 32], P('visit', 'bulk'), may hold values from 0 to 15
- piece_extent: int32 [8, 32, 32, 2], P('visit', 'bulk'), may hold values from 64 to 128
- basis: float32 [4, 128, 128], replicated, may hold values from -0.046875 to 0.046875
- coeffs: float32 [8, 4], P('visit'), may hold values from -4 to 4
Outputs:
- coadd: float32 [8192, 1024], P('bulk', 'visit')
- weight_map: float32 [8192, 1024], P('bulk', 'visit')
Inputs may be any that keep to these rules, and one draw needn't show every extreme that they name: `piece_owner`: among the pieces on one device, no owner is named by more than 2 pieces, a bound that some block reaches. `warp_rows`: entries are nonnegative and each row sums to one. `warp_cols`: entries are nonnegative and each row sums to one.
All inputs are finite; a program needn't handle non-finite values.
Results may differ from a plain program's by a relative error of at most 0.0003.
Values sent between devices are 32-bit elements; how exact they have to be, the bound alone decides.
A program may use at most 128 MiB of HBM per device.

v0:
```python
import numpy as np

import jax
import jax.numpy as jnp
from jax import lax
from jax.experimental import pallas as pl
from jax.experimental.pallas import tpu as pltpu
from jax.sharding import PartitionSpec as P

MESH = pl.DeviceIdType.MESH
F32 = jnp.float32
BF16 = jnp.bfloat16

S = 128
HALO = 64
BR = 2
BC = 8
CAP = 2
VISITS = 8
OWNERS = 32
PIECES = 32
BLOCKS = BR * BC
SLOTS = OWNERS * CAP
LEN = 256
WIDE = (BC + 1) * S
TALL = BR * S + 2 * HALO
STRIDE = 11


def split_np(table):
    table = table.astype(np.float32)
    high = table.astype(jnp.bfloat16)
    low = (table - high.astype(np.float32)).astype(jnp.bfloat16)
    return high, low


def dft_tables():
    freq = (np.arange(LEN // 2) + 0.5) * (2.0 * np.pi / LEN)
    places = np.arange(LEN)
    taps = np.arange(-HALO, HALO)
    full = np.concatenate([np.cos(freq[:, None] * places), np.sin(freq[:, None] * places)])
    kern = np.concatenate([np.cos(freq[:, None] * taps), np.sin(freq[:, None] * taps)])
    mid = full[:, HALO : HALO + S] / (LEN // 2)
    return [
        part
        for table in (full, full.T, mid, mid.T, kern, kern.T)
        for part in split_np(np.ascontiguousarray(table))
    ]


def split(x):
    high = x.astype(BF16)
    return high, (x - high.astype(F32)).astype(BF16)


NN = (((1,), (0,)), ((), ()))
NT = (((1,), (1,)), ((), ()))


def dot3(a, b, dims=NN):
    def one(p, q):
        return lax.dot_general(p, q, dims, preferred_element_type=F32)

    return one(a[0], b[0]) + (one(a[0], b[1]) + one(a[1], b[0]))


def kernel(
    tab_ref, coef_ref, flux_hbm, ivar_hbm, rows_hbm, cols_hbm, ids_ref, basis_ref,
    full_h, full_l, fullt_h, fullt_l, mid_h, mid_l, midt_h, midt_l,
    kern_h, kern_l, kernt_h, kernt_l,
    coadd_ref, weight_ref,
    flux_v, ivar_v, rows_v, cols_v, send, recv, ids_recv, canvas, image,
    vh, vl, fxh, fxl, spec, numer, own_out, land,
    in_sem, ids_send_sem, ids_recv_sem, send_sem, recv_sem, chain_send, chain_recv, halo_send, halo_recv,
):
    v = lax.axis_index("visit")
    b = lax.axis_index("bulk")
    x, y, c = b // 8, (b // 2) % 4, b % 2

    def device_at(step, sign):
        dx, dy, dc = step // 8, (step // 2) % 4, step % 2
        if sign < 0:
            dx, dy = 4 - dx, 4 - dy
        return ((x + dx) % 4 * 4 + (y + dy) % 4) * 2 + (c + dc) % 2

    right, left = (v + 1) % VISITS, (v + VISITS - 1) % VISITS

    loads = [
        pltpu.make_async_copy(src, dst, in_sem.at[k])
        for k, (src, dst) in enumerate(
            ((flux_hbm, flux_v), (ivar_hbm, ivar_v), (rows_hbm, rows_v), (cols_hbm, cols_v))
        )
    ]
    for load in loads:
        load.start()
    barrier = pltpu.get_barrier_semaphore()

    def greet(i, carry):
        pl.semaphore_signal(barrier, inc=1, device_id=(v, device_at(i, 1)), device_id_type=MESH)
        return carry

    lax.fori_loop(1, OWNERS, greet, 0)
    for z in (right, left):
        pl.semaphore_signal(barrier, inc=1, device_id=(z, b), device_id_type=MESH)

    def clear(i, carry):
        canvas[0, i] = jnp.zeros((S, S), F32)
        canvas[1, i] = jnp.zeros((S, S), F32)
        return carry

    lax.fori_loop(0, BLOCKS, clear, 0)

    @pl.when(b == 0)
    def _():
        image[0:HALO, :] = jnp.zeros((HALO, WIDE), F32)

    @pl.when(b == OWNERS - 1)
    def _():
        image[HALO + BR * S : TALL, :] = jnp.zeros((HALO, WIDE), F32)

    for load in loads:
        load.wait()
    pl.semaphore_wait(barrier, OWNERS - 1 + 2)

    def id_copy(i):
        to = device_at(i, 1)
        return pltpu.make_async_remote_copy(
            src_ref=ids_ref.at[to], dst_ref=ids_recv.at[i], send_sem=ids_send_sem.at[i],
            recv_sem=ids_recv_sem.at[i], device_id=(v, to), device_id_type=MESH)

    def plane_copy(plane, i):
        return pltpu.make_async_remote_copy(
            src_ref=send.at[plane, i], dst_ref=recv.at[plane, i], send_sem=send_sem.at[plane, i],
            recv_sem=recv_sem.at[plane, i], device_id=(v, device_at(i, 1)), device_id_type=MESH)

    row_at = lax.broadcasted_iota(jnp.int32, (S, S), 0)
    col_at = lax.broadcasted_iota(jnp.int32, (S, S), 1)

    def warp_slot(i, r):
        slot = device_at(i, 1) * CAP + r
        piece = tab_ref[slot]
        ok = (row_at < tab_ref[SLOTS + slot]) & (col_at < tab_ref[2 * SLOTS + slot])
        weighted = jnp.where(ok, ivar_v[piece], 0.0)
        both = jnp.concatenate([weighted * flux_v[piece], weighted], axis=1)
        half = dot3(split(rows_v[piece]), split(both))
        tall = jnp.concatenate([half[:, :S], half[:, S:]], axis=0)
        warped = dot3(split(tall), split(cols_v[piece]), NT)
        send[0, i, r] = warped[:S]
        send[1, i, r] = warped[S:]

    def warp_step(k, carry):
        i = (k * STRIDE) % OWNERS
        for r in range(CAP):
            warp_slot(i, r)

        id_copy(i).start()
        plane_copy(1, i).start()
        return carry

    lax.fori_loop(1, OWNERS, warp_step, 0)

    def flux_step(k, carry):
        plane_copy(0, (k * STRIDE) % OWNERS).start()
        return carry

    lax.fori_loop(1, OWNERS, flux_step, 0)
    for r in range(CAP):
        warp_slot(0, r)

    taps = coef_ref[0] * basis_ref[0]
    for k in range(1, 4):
        taps = taps + coef_ref[k] * basis_ref[k]
    half_spec = dot3((kern_h[...], kern_l[...]), split(taps))
    spec[...] = dot3(split(half_spec), (kernt_h[...], kernt_l[...]))

    def add_slots(plane, id_rows, source, i):
        for r in range(CAP):
            pass
        first = jnp.broadcast_to(id_rows[0:1, :], (8, S))
        second = jnp.broadcast_to(id_rows[1:2, :], (8, S))

        def rows_step(q, carry):
            at = pl.ds(pl.multiple_of(q * 8, 8), 8)
            one = source[plane, i, 0, at, :]
            two = source[plane, i, 1, at, :]
            for block in range(BLOCKS):
                canvas[plane, block, at, :] = canvas[plane, block, at, :] + (
                    jnp.where(first == float(block), one, 0.0)
                    + jnp.where(second == float(block), two, 0.0))
            return carry

        lax.fori_loop(0, S // 8, rows_step, 0)

    add_slots(1, ids_ref[b], send, 0)

    def ivar_in(k, carry):
        i = (k * STRIDE) % OWNERS
        id_copy(i).wait_recv()
        plane_copy(1, i).wait_recv()
        add_slots(1, ids_recv[i], recv, i)
        return carry

    lax.fori_loop(1, OWNERS, ivar_in, 0)

    def chunk_of(direction, step):
        return (v + 4 - step) % VISITS if direction == 0 else (v + 4 + step) % VISITS

    def chain_copy(what, direction, step, half):
        return pltpu.make_async_remote_copy(
            src_ref=own_out.at[what, direction, step, half], dst_ref=land.at[what, direction, step, half],
            send_sem=chain_send.at[what, direction, step, half],
            recv_sem=chain_recv.at[what, direction, step, half],
            device_id=(right if direction == 0 else left, b), device_id_type=MESH)

    def chain_first(what, own):
        for direction in (0, 1):
            own_out[what, direction, 0, direction] = own(direction, chunk_of(direction, 0))
            chain_copy(what, direction, 0, direction).start()

    def chain_step(what, step, own):
        for near in (0, 1):
            for direction in (0, 1):
                half = direction if near == 0 else 1 - direction
                value = own(half, chunk_of(direction, step))
                if step > 1 or half == direction:
                    chain_copy(what, direction, step - 1, half).wait_recv()
                    value = value + land[what, direction, step - 1, half]
                own_out[what, direction, step, half] = value
                chain_copy(what, direction, step, half).start()

    def chain_last(what, half, own):
        for direction in (0, 1):
            chain_copy(what, direction, 3, half).wait_recv()
        return own(half, v) + (land[what, 0, 3, half] + land[what, 1, 3, half])

    def ivar_own(half, chunk):
        return canvas[1, half * BC + chunk]

    chain_first(1, ivar_own)
    add_slots(0, ids_ref[b], send, 0)

    def flux_in(k, carry):
        i = (k * STRIDE) % OWNERS
        plane_copy(0, i).wait_recv()
        add_slots(0, ids_recv[i], recv, i)
        return carry

    lax.fori_loop(1, 8, flux_in, 0)
    chain_step(1, 1, ivar_own)
    lax.fori_loop(8, 16, flux_in, 0)
    chain_step(1, 2, ivar_own)
    lax.fori_loop(16, 23, flux_in, 0)
    chain_step(1, 3, ivar_own)
    lax.fori_loop(23, 30, flux_in, 0)
    for half in range(BR):
        weight_ref[half * S : half * S + S, :] = chain_last(1, half, ivar_own)
    lax.fori_loop(30, OWNERS, flux_in, 0)

    for br in range(BR):
        before = jnp.zeros((S, HALO), F32)
        for j in range(BC + 1):
            if j < BC:
                cur = canvas[0, br * BC + j] / jnp.maximum(canvas[1, br * BC + j], 1.0)
                piece = jnp.concatenate([before, cur[:, :HALO]], axis=1)
                before = cur[:, HALO:]
            else:
                piece = jnp.concatenate([before, jnp.zeros((S, HALO), F32)], axis=1)
            image[HALO + br * S : HALO + br * S + S, j * S : j * S + S] = piece

    def halo_copy(side):
        start, to = (BR * S, 0) if side == 0 else (HALO, HALO + BR * S)
        return pltpu.make_async_remote_copy(
            src_ref=image.at[start : start + HALO, :], dst_ref=image.at[to : to + HALO, :],
            send_sem=halo_send.at[side], recv_sem=halo_recv.at[side],
            device_id=(v, (b + 1) % OWNERS if side == 0 else (b + OWNERS - 1) % OWNERS),
            device_id_type=MESH)

    has_next, has_before = b < OWNERS - 1, b > 0

    @pl.when(has_next)
    def _():
        halo_copy(0).start()

    @pl.when(has_before)
    def _():
        halo_copy(1).start()

    mine = slice(HALO, HALO + BR * S)
    vh[mine, :], vl[mine, :] = split(image[mine, :])

    @pl.when(has_before)
    def _():
        halo_copy(0).wait_recv()

    @pl.when(has_next)
    def _():
        halo_copy(1).wait_recv()

    for top in (0, HALO + BR * S):
        edge = slice(top, top + HALO)
        vh[edge, :], vl[edge, :] = split(image[edge, :])

    def row_stage(j, carry):
        at = pl.ds(pl.multiple_of(j * S, S), S)
        for rt in range(BR):
            here = slice(rt * S, rt * S + LEN)
            out = dot3((full_h[...], full_l[...]), (vh[here, at], vl[here, at]))
            there = slice(rt * LEN, rt * LEN + LEN)
            fxh[there, at], fxl[there, at] = split(out)
        return carry

    lax.fori_loop(0, BC + 1, row_stage, 0)

    def tile(bc):
        at = pl.ds(pl.multiple_of(bc * S, S), LEN)
        kcc, kcs = spec[:S, :S], spec[:S, S:]
        ksc, kss = spec[S:, :S], spec[S:, S:]
        for rt in range(BR):
            there = slice(rt * LEN, rt * LEN + LEN)
            freq = dot3((fxh[there, at], fxl[there, at]), (fullt_h[...], fullt_l[...]))
            xcc, xcs = freq[:S, :S], freq[:S, S:]
            xsc, xss = freq[S:, :S], freq[S:, S:]
            ycc = (xcc * kcc - xcs * kcs) - (xsc * ksc - xss * kss)
            ycs = (xcc * kcs + xcs * kcc) - (xsc * kss + xss * ksc)
            ysc = (xcc * ksc - xcs * kss) + (xsc * kcc - xss * kcs)
            yss = (xcc * kss + xcs * ksc) + (xsc * kcs + xss * kcc)
            prod = jnp.concatenate(
                [jnp.concatenate([ycc, ycs], axis=1), jnp.concatenate([ysc, yss], axis=1)], axis=0)
            back = dot3(split(prod), (mid_h[...], mid_l[...]))
            matched = dot3((midt_h[...], midt_l[...]), split(back))
            numer[rt, bc] = canvas[1, rt * BC + bc] * matched

    def numer_own(half, chunk):
        return numer[half, chunk]

    def tile_step(k, carry):
        near = (k + 1) // 2
        tile((v + 4 + jnp.where(k % 2 == 0, near, VISITS - near)) % VISITS)

        @pl.when(k == 0)
        def _():
            chain_first(0, numer_own)

        for step in (1, 2, 3):
            @pl.when(k == 2 * step)
            def _(step=step):
                chain_step(0, step, numer_own)

        return carry

    lax.fori_loop(0, VISITS, tile_step, 0)
    for half in range(BR):
        at = slice(half * S, half * S + S)
        coadd_ref[at, :] = chain_last(0, half, numer_own) / jnp.maximum(weight_ref[at, :], 1.0)

    def drain(i, carry):
        id_copy(i).wait_send()
        plane_copy(0, i).wait_send()
        plane_copy(1, i).wait_send()
        return carry

    lax.fori_loop(1, OWNERS, drain, 0)
    for what in (0, 1):
        for direction in (0, 1):
            chain_copy(what, direction, 0, direction).wait_send()
            for step in (1, 2, 3):
                for half in (0, 1):
                    chain_copy(what, direction, step, half).wait_send()

    @pl.when(has_next)
    def _():
        halo_copy(0).wait_send()

    @pl.when(has_before)
    def _():
        halo_copy(1).wait_send()


def on_device(piece_flux, piece_ivar, warp_rows, warp_cols, piece_owner, piece_slot, piece_extent, basis, coeffs):
    owner = piece_owner.reshape(PIECES)
    slot_id = piece_slot.reshape(PIECES)
    extent = piece_extent.reshape(PIECES, 2)
    order = jnp.arange(PIECES, dtype=jnp.int32)
    earlier = (owner[:, None] == owner[None, :]) & (order[None, :] < order[:, None])
    dest = owner * CAP + jnp.sum(earlier.astype(jnp.int32), axis=1)
    hit = dest[:, None] == jnp.arange(SLOTS, dtype=jnp.int32)[None, :]
    facts = jnp.stack([order, extent[:, 0], extent[:, 1], slot_id + 1])
    table = jnp.sum(jnp.where(hit[None], facts[:, :, None], 0), axis=1)
    ids = (table[3] - 1).astype(F32).reshape(OWNERS, CAP, 1)
    ids = jnp.broadcast_to(ids, (OWNERS, CAP, S))
    shape = (PIECES, S, S)
    vmem = pl.BlockSpec(memory_space=pltpu.VMEM)
    smem = pl.BlockSpec(memory_space=pltpu.SMEM)
    hbm = pl.BlockSpec(memory_space=pl.ANY)
    tables = dft_tables()
    dma = pltpu.SemaphoreType.DMA
    coadd, weight = pl.pallas_call(
        kernel,
        out_shape=[jax.ShapeDtypeStruct((BR * S, S), F32)] * 2,
        in_specs=[smem, smem, hbm, hbm, hbm, hbm] + [vmem] * (2 + len(tables)),
        out_specs=[vmem, vmem],
        scratch_shapes=[pltpu.VMEM(shape, F32)] * 4
        + [
            pltpu.VMEM((2, OWNERS, CAP, S, S), F32),
            pltpu.VMEM((2, OWNERS, CAP, S, S), F32),
            pltpu.VMEM((OWNERS, CAP, S), F32),
            pltpu.VMEM((2, BLOCKS, S, S), F32),
            pltpu.VMEM((TALL, WIDE), F32),
            pltpu.VMEM((TALL, WIDE), BF16),
            pltpu.VMEM((TALL, WIDE), BF16),
            pltpu.VMEM((BR * LEN, WIDE), BF16),
            pltpu.VMEM((BR * LEN, WIDE), BF16),
            pltpu.VMEM((LEN, LEN), F32),
            pltpu.VMEM((BR, BC, S, S), F32),
            pltpu.VMEM((2, 2, 4, 2, S, S), F32),
            pltpu.VMEM((2, 2, 4, 2, S, S), F32),
            dma((4,)),
            dma((OWNERS,)),
            dma((OWNERS,)),
            dma((2, OWNERS)),
            dma((2, OWNERS)),
            dma((2, 2, 4, 2)),
            dma((2, 2, 4, 2)),
            dma((2,)),
            dma((2,)),
        ],
        compiler_params=pltpu.CompilerParams(
            collective_id=0, has_side_effects=True, vmem_limit_bytes=60 * 1024 * 1024
        ),
        name="coadd",
    )(
        table[:3].reshape(3 * SLOTS), coeffs.reshape(4),
        piece_flux.reshape(shape), piece_ivar.reshape(shape), warp_rows.reshape(shape), warp_cols.reshape(shape),
        ids, basis, *[jnp.asarray(t) for t in tables],
    )
    return coadd, weight


def solution(mesh):
    piece = P("visit", "bulk", None, None, None)
    return jax.shard_map(
        on_device,
        mesh=mesh,
        in_specs=(piece, piece, piece, piece, P("visit", "bulk", None, None), P("visit", "bulk", None),
                  P("visit", "bulk", None, None), P(), P("visit", None)),
        out_specs=(P("bulk", "visit"), P("bulk", "visit")),
        check_vma=False,
    )
```

profile of v0, /device:TPU:24, one launch (start us, length us, event | category | flops | bytes accessed | tf_op | source)
XLA Modules:
  0.0 156.1 jit_solution(2004789740041479819)
XLA Ops:
  0.6 0.7 add_bitcast_fusion
  1.3 0.9 convert_reduce_fusion
  2.2 0.7 multiply_add_fusion
  2.9 0.8 slice_bitcast_fusion.1
  3.6 0.1 iota_compare_fusion
  3.7 0.1 select_reduce_fusion
  3.8 0.6 reshape.83.tab_ref
  4.5 0.1 convert_element_type.15
  4.6 0.7 broadcast_in_dim.34.ids_ref
  5.3 147.6 %coadd.1 = (f32[256,128]{1,0:T(8,128)}, f32[256,128]{1,0:T(8,128)}) custom-call(s32[192]{0:T(256)} %reshape.83.tab_ref, f32[4]{0:T(128)} %bitcast.21, f32[32,128,128]{2,1,0:T(8,128)} %bitcast.15, f32[32,128,128]{2,1,0:T(8,128)} %bitcast.16, f32[32,128,128]{2,1,0:T(8,128)} %bitcast.17, f32[32,128,128]{2,1,0:T(8,128)} %bitcast.18, ...), custom_call_target="tpu_custom_call" | custom-call | tf_op jit(solution)/shard_map/coadd/pallas_call | solution.py:397
  152.9 1.6 %copy.25 = f32[256,128]{1,0:T(8,128)} copy(f32[256,128]{1,0:T(8,128)} %get-tuple-element.6) | data formatting | bytes 262144
  154.5 1.6 %copy.26 = f32[256,128]{1,0:T(8,128)} copy(f32[256,128]{1,0:T(8,128)} %get-tuple-element.7) | data formatting | bytes 262144
  (3 shorter events, 0.0 us)
where the time goes:
time: 156 us
  Pallas kernels  148 us (95%)
  local copies, waits for them, and re-layouts  5.35 us (3%)
  other arithmetic  2.44 us (2%)
    pallas_call x1, Pallas kernels, on_device(): pl.pallas_call(kernel, out_shape=[jax.ShapeDtypeStruct((BR * S, S), F32)]...  148 us
    unnamed x2, local copies, waits for them, and re-layouts  3.14 us

commit v1 on v0

--- a/solution.py
+++ b/solution.py
@@ -20,7 +20,7 @@
 OWNERS = 32
 PIECES = 32
 BLOCKS = BR * BC
-SLOTS = OWNERS * CAP
+PART = S // 2
 LEN = 256
 WIDE = (BC + 1) * S
 TALL = BR * S + 2 * HALO
@@ -65,22 +65,20 @@
 
 
 def kernel(
-    tab_ref, coef_ref, flux_hbm, ivar_hbm, rows_hbm, cols_hbm, ids_ref, basis_ref,
+    first_ref, last_ref, slot_ref, extent_ref, coef_ref, flux_hbm, ivar_hbm, rows_hbm, cols_hbm, basis_ref,
     full_h, full_l, fullt_h, fullt_l, mid_h, mid_l, midt_h, midt_l,
     kern_h, kern_l, kernt_h, kernt_l,
     coadd_ref, weight_ref,
-    flux_v, ivar_v, rows_v, cols_v, send, recv, ids_recv, canvas, image,
+    flux_v, ivar_v, rows_v, cols_v, send, recv, ids_own, ids_recv, dense, passed, arrived, canvas, image,
     vh, vl, fxh, fxl, spec, numer, own_out, land,
-    in_sem, ids_send_sem, ids_recv_sem, send_sem, recv_sem, chain_send, chain_recv, halo_send, halo_recv,
+    in_sem, ids_send_sem, ids_recv_sem, send_sem, recv_sem, pass_send, pass_recv,
+    chain_send, chain_recv, halo_send, halo_recv,
 ):
     v = lax.axis_index("visit")
     b = lax.axis_index("bulk")
     x, y, c = b // 8, (b // 2) % 4, b % 2
 
-    def device_at(step, sign):
-        dx, dy, dc = step // 8, (step // 2) % 4, step % 2
-        if sign < 0:
-            dx, dy = 4 - dx, 4 - dy
+    def device_at(dx, dy, dc):
         return ((x + dx) % 4 * 4 + (y + dy) % 4) * 2 + (c + dc) % 2
 
     right, left = (v + 1) % VISITS, (v + VISITS - 1) % VISITS
@@ -96,19 +94,35 @@
     barrier = pltpu.get_barrier_semaphore()
 
     def greet(i, carry):
-        pl.semaphore_signal(barrier, inc=1, device_id=(v, device_at(i, 1)), device_id_type=MESH)
+        pl.semaphore_signal(barrier, inc=1, device_id=(v, (b + i) % OWNERS), device_id_type=MESH)
         return carry
 
     lax.fori_loop(1, OWNERS, greet, 0)
     for z in (right, left):
         pl.semaphore_signal(barrier, inc=1, device_id=(z, b), device_id_type=MESH)
 
-    def clear(i, carry):
-        canvas[0, i] = jnp.zeros((S, S), F32)
-        canvas[1, i] = jnp.zeros((S, S), F32)
-        return carry
-
-    lax.fori_loop(0, BLOCKS, clear, 0)
+    def line_device(route, j):
+        return jnp.where(route == 0, device_at(j // 2, 0, j % 2), device_at(0, j // 2, j % 2))
+
+    def owner_at(route, j, e):
+        return jnp.where(route == 0, device_at(j // 2, e, j % 2), device_at(e, j // 2, j % 2))
+
+    tile_row = lax.broadcasted_iota(jnp.int32, (8, S), 0)
+
+    def make_ids(n, carry):
+        route, j = n // 8, n % 8
+        rows = jnp.zeros((8, S), F32)
+        for e in range(4):
+            owner = owner_at(route, j, e)
+            low, high = first_ref[owner], last_ref[owner]
+            one = jnp.where(high >= 0, slot_ref[jnp.minimum(low, PIECES - 1)], -1)
+            two = jnp.where(high > low, slot_ref[jnp.maximum(high, 0)], -1)
+            rows = jnp.where(tile_row == 2 * e, one.astype(F32), rows)
+            rows = jnp.where(tile_row == 2 * e + 1, two.astype(F32), rows)
+        ids_own[route, j] = rows
+        return carry
+
+    lax.fori_loop(0, 16, make_ids, 0)
 
     @pl.when(b == 0)
     def _():
@@ -122,45 +136,68 @@
         load.wait()
     pl.semaphore_wait(barrier, OWNERS - 1 + 2)
 
-    def id_copy(i):
-        to = device_at(i, 1)
+    def id_copy(route, j):
         return pltpu.make_async_remote_copy(
-            src_ref=ids_ref.at[to], dst_ref=ids_recv.at[i], send_sem=ids_send_sem.at[i],
-            recv_sem=ids_recv_sem.at[i], device_id=(v, to), device_id_type=MESH)
-
-    def plane_copy(plane, i):
+            src_ref=ids_own.at[route, j], dst_ref=ids_recv.at[route, j], send_sem=ids_send_sem.at[route, j],
+            recv_sem=ids_recv_sem.at[route, j], device_id=(v, line_device(route, j)), device_id_type=MESH)
+
+    def part_copy(plane, route, j, e):
         return pltpu.make_async_remote_copy(
-            src_ref=send.at[plane, i], dst_ref=recv.at[plane, i], send_sem=send_sem.at[plane, i],
-            recv_sem=recv_sem.at[plane, i], device_id=(v, device_at(i, 1)), device_id_type=MESH)
+            src_ref=send.at[plane, route, j, e], dst_ref=recv.at[plane, route, j, e],
+            send_sem=send_sem.at[plane, route, j], recv_sem=recv_sem.at[plane, route, j],
+            device_id=(v, line_device(route, j)), device_id_type=MESH)
+
+    def line_copy(plane, route, j):
+        return pltpu.make_async_remote_copy(
+            src_ref=send.at[plane, route, j], dst_ref=recv.at[plane, route, j],
+            send_sem=send_sem.at[plane, route, j], recv_sem=recv_sem.at[plane, route, j],
+            device_id=(v, line_device(route, j)), device_id_type=MESH)
+
+    def send_ids(n, carry):
+        id_copy(n % 2, n // 2).start()
+        return carry
+
+    lax.fori_loop(2, 16, send_ids, 0)
 
     row_at = lax.broadcasted_iota(jnp.int32, (S, S), 0)
     col_at = lax.broadcasted_iota(jnp.int32, (S, S), 1)
 
     def warp_slot(i, r):
-        slot = device_at(i, 1) * CAP + r
-        piece = tab_ref[slot]
-        ok = (row_at < tab_ref[SLOTS + slot]) & (col_at < tab_ref[2 * SLOTS + slot])
+        dx, dy, dc = i // 8, (i // 2) % 4, i % 2
+        owner = device_at(dx, dy, dc)
+        piece = jnp.minimum(first_ref[owner], PIECES - 1) if r == 0 else jnp.maximum(last_ref[owner], 0)
+        ok = (row_at < extent_ref[0, piece]) & (col_at < extent_ref[1, piece])
         weighted = jnp.where(ok, ivar_v[piece], 0.0)
         both = jnp.concatenate([weighted * flux_v[piece], weighted], axis=1)
         half = dot3(split(rows_v[piece]), split(both))
         tall = jnp.concatenate([half[:, :S], half[:, S:]], axis=0)
         warped = dot3(split(tall), split(cols_v[piece]), NT)
-        send[0, i, r] = warped[:S]
-        send[1, i, r] = warped[S:]
+        for plane in (0, 1):
+            send[plane, 0, dx * 2 + dc, dy, r] = warped[plane * S : plane * S + PART]
+            send[plane, 1, dy * 2 + dc, dx, r] = warped[plane * S + PART : plane * S + S]
+
+    def send_parts(plane, i):
+        dx, dy, dc = i // 8, (i // 2) % 4, i % 2
+
+        @pl.when(dx + dc > 0)
+        def _():
+            part_copy(plane, 0, dx * 2 + dc, dy).start()
+
+        @pl.when(dy + dc > 0)
+        def _():
+            part_copy(plane, 1, dy * 2 + dc, dx).start()
 
     def warp_step(k, carry):
         i = (k * STRIDE) % OWNERS
         for r in range(CAP):
             warp_slot(i, r)
-
-        id_copy(i).start()
-        plane_copy(1, i).start()
+        send_parts(1, i)
         return carry
 
     lax.fori_loop(1, OWNERS, warp_step, 0)
 
     def flux_step(k, carry):
-        plane_copy(0, (k * STRIDE) % OWNERS).start()
+        send_parts(0, (k * STRIDE) % OWNERS)
         return carry
 
     lax.fori_loop(1, OWNERS, flux_step, 0)
@@ -173,34 +210,100 @@
     half_spec = dot3((kern_h[...], kern_l[...]), split(taps))
     spec[...] = dot3(split(half_spec), (kernt_h[...], kernt_l[...]))
 
-    def add_slots(plane, id_rows, source, i):
-        for r in range(CAP):
-            pass
-        first = jnp.broadcast_to(id_rows[0:1, :], (8, S))
-        second = jnp.broadcast_to(id_rows[1:2, :], (8, S))
+    def add_line(plane, route, j, source, ids, fresh):
+        marks = ids[route, j]
 
         def rows_step(q, carry):
             at = pl.ds(pl.multiple_of(q * 8, 8), 8)
-            one = source[plane, i, 0, at, :]
-            two = source[plane, i, 1, at, :]
-            for block in range(BLOCKS):
-                canvas[plane, block, at, :] = canvas[plane, block, at, :] + (
-                    jnp.where(first == float(block), one, 0.0)
-                    + jnp.where(second == float(block), two, 0.0))
+            for e in range(4):
+                first = jnp.broadcast_to(marks[2 * e : 2 * e + 1, :], (8, S))
+                second = jnp.broadcast_to(marks[2 * e + 1 : 2 * e + 2, :], (8, S))
+                one = source[plane, route, j, e, 0, at, :]
+                two = source[plane, route, j, e, 1, at, :]
+                for block in range(BLOCKS):
+                    value = jnp.where(first == float(block), one, 0.0) + jnp.where(second == float(block), two, 0.0)
+                    if not fresh:
+                        value = dense[plane, route, e, block, at, :] + value
+                    dense[plane, route, e, block, at, :] = value
             return carry
 
-        lax.fori_loop(0, S // 8, rows_step, 0)
-
-    add_slots(1, ids_ref[b], send, 0)
-
-    def ivar_in(k, carry):
-        i = (k * STRIDE) % OWNERS
-        id_copy(i).wait_recv()
-        plane_copy(1, i).wait_recv()
-        add_slots(1, ids_recv[i], recv, i)
-        return carry
-
-    lax.fori_loop(1, OWNERS, ivar_in, 0)
+        lax.fori_loop(0, PART // 8, rows_step, 0)
+
+    def add_plane(plane):
+        def own(n, carry):
+            add_line(plane, n, 0, send, ids_own, True)
+            return carry
+
+        def landed(n, carry):
+            route, j = n % 2, n // 2
+            line_copy(plane, route, j).wait_recv()
+            add_line(plane, route, j, recv, ids_recv, False)
+            return carry
+
+        lax.fori_loop(0, 2, own, 0)
+        lax.fori_loop(2, 16, landed, 0)
+
+    LOW, HIGH = slice(0, BLOCKS // 2), slice(BLOCKS // 2, BLOCKS)
+
+    def pass_copy(plane, route, m):
+        ahead = m % 2 == 0
+        step = 1 if ahead else 3
+        to = device_at(0, step, 0) if route == 0 else device_at(step, 0, 0)
+        way = 0 if ahead else 1
+        if m < 2:
+            src = dense.at[plane, route, 2, LOW if ahead else HIGH]
+            dst = passed.at[plane, route, way]
+        else:
+            part = (HIGH if ahead else LOW) if m < 4 else (LOW if ahead else HIGH)
+            src = dense.at[plane, route, step, part]
+            dst = arrived.at[plane, route, way, part]
+        return pltpu.make_async_remote_copy(
+            src_ref=src, dst_ref=dst, send_sem=pass_send.at[plane, route, m], recv_sem=pass_recv.at[plane, route, m],
+            device_id=(v, to), device_id_type=MESH)
+
+    def pass_first(plane):
+        for m in range(4):
+            for route in (0, 1):
+                pass_copy(plane, route, m).start()
+
+    def pass_merged(plane):
+        for m in (4, 5):
+            for route in (0, 1):
+                pass_copy(plane, route, m - 4).wait_recv()
+
+                def merge(block, carry, m=m, route=route):
+                    there = block if m == 4 else block + BLOCKS // 2
+                    step = 1 if m == 4 else 3
+                    dense[plane, route, step, there] = dense[plane, route, step, there] + passed[plane, route, m - 4, block]
+                    return carry
+
+                lax.fori_loop(0, BLOCKS // 2, merge, 0)
+                pass_copy(plane, route, m).start()
+
+    def pass_last(plane):
+        for route in (0, 1):
+            for m in (2, 3, 4, 5):
+                pass_copy(plane, route, m).wait_recv()
+            rows = slice(route * PART, route * PART + PART)
+
+            def total(block, carry, route=route, rows=rows):
+                canvas[plane, block, rows, :] = dense[plane, route, 0, block] + (
+                    arrived[plane, route, 0, block] + arrived[plane, route, 1, block])
+                return carry
+
+            lax.fori_loop(0, BLOCKS, total, 0)
+
+    def ids_in(n, carry):
+        id_copy(n % 2, n // 2).wait_recv()
+        return carry
+
+    lax.fori_loop(2, 16, ids_in, 0)
+    add_plane(1)
+    pass_first(1)
+    add_plane(0)
+    pass_merged(1)
+    pass_first(0)
+    pass_last(1)
 
     def chunk_of(direction, step):
         return (v + 4 - step) % VISITS if direction == 0 else (v + 4 + step) % VISITS
@@ -237,24 +340,10 @@
         return canvas[1, half * BC + chunk]
 
     chain_first(1, ivar_own)
-    add_slots(0, ids_ref[b], send, 0)
-
-    def flux_in(k, carry):
-        i = (k * STRIDE) % OWNERS
-        plane_copy(0, i).wait_recv()
-        add_slots(0, ids_recv[i], recv, i)
-        return carry
-
-    lax.fori_loop(1, 8, flux_in, 0)
-    chain_step(1, 1, ivar_own)
-    lax.fori_loop(8, 16, flux_in, 0)
-    chain_step(1, 2, ivar_own)
-    lax.fori_loop(16, 23, flux_in, 0)
-    chain_step(1, 3, ivar_own)
-    lax.fori_loop(23, 30, flux_in, 0)
-    for half in range(BR):
-        weight_ref[half * S : half * S + S, :] = chain_last(1, half, ivar_own)
-    lax.fori_loop(30, OWNERS, flux_in, 0)
+    pass_merged(0)
+    for step in (1, 2, 3):
+        chain_step(1, step, ivar_own)
+    pass_last(0)
 
     for br in range(BR):
         before = jnp.zeros((S, HALO), F32)
@@ -287,6 +376,8 @@
 
     mine = slice(HALO, HALO + BR * S)
     vh[mine, :], vl[mine, :] = split(image[mine, :])
+    for half in range(BR):
+        weight_ref[half * S : half * S + S, :] = chain_last(1, half, ivar_own)
 
     @pl.when(has_before)
     def _():
@@ -353,13 +444,18 @@
         at = slice(half * S, half * S + S)
         coadd_ref[at, :] = chain_last(0, half, numer_own) / jnp.maximum(weight_ref[at, :], 1.0)
 
-    def drain(i, carry):
-        id_copy(i).wait_send()
-        plane_copy(0, i).wait_send()
-        plane_copy(1, i).wait_send()
-        return carry
-
-    lax.fori_loop(1, OWNERS, drain, 0)
+    def drain(n, carry):
+        route, j = n % 2, n // 2
+        id_copy(route, j).wait_send()
+        line_copy(0, route, j).wait_send()
+        line_copy(1, route, j).wait_send()
+        return carry
+
+    lax.fori_loop(2, 16, drain, 0)
+    for plane in (0, 1):
+        for route in (0, 1):
+            for m in range(6):
+                pass_copy(plane, route, m).wait_send()
     for what in (0, 1):
         for direction in (0, 1):
             chain_copy(what, direction, 0, direction).wait_send()
@@ -378,16 +474,10 @@
 
 def on_device(piece_flux, piece_ivar, warp_rows, warp_cols, piece_owner, piece_slot, piece_extent, basis, coeffs):
     owner = piece_owner.reshape(PIECES)
-    slot_id = piece_slot.reshape(PIECES)
-    extent = piece_extent.reshape(PIECES, 2)
     order = jnp.arange(PIECES, dtype=jnp.int32)
-    earlier = (owner[:, None] == owner[None, :]) & (order[None, :] < order[:, None])
-    dest = owner * CAP + jnp.sum(earlier.astype(jnp.int32), axis=1)
-    hit = dest[:, None] == jnp.arange(SLOTS, dtype=jnp.int32)[None, :]
-    facts = jnp.stack([order, extent[:, 0], extent[:, 1], slot_id + 1])
-    table = jnp.sum(jnp.where(hit[None], facts[:, :, None], 0), axis=1)
-    ids = (table[3] - 1).astype(F32).reshape(OWNERS, CAP, 1)
-    ids = jnp.broadcast_to(ids, (OWNERS, CAP, S))
+    hit = owner[:, None] == jnp.arange(OWNERS, dtype=jnp.int32)[None, :]
+    first = jnp.min(jnp.where(hit, order[:, None], PIECES), axis=0)
+    last = jnp.max(jnp.where(hit, order[:, None], -1), axis=0)
     shape = (PIECES, S, S)
     vmem = pl.BlockSpec(memory_space=pltpu.VMEM)
     smem = pl.BlockSpec(memory_space=pltpu.SMEM)
@@ -397,13 +487,17 @@
     coadd, weight = pl.pallas_call(
         kernel,
         out_shape=[jax.ShapeDtypeStruct((BR * S, S), F32)] * 2,
-        in_specs=[smem, smem, hbm, hbm, hbm, hbm] + [vmem] * (2 + len(tables)),
+        in_specs=[smem] * 5 + [hbm] * 4 + [vmem] * (1 + len(tables)),
         out_specs=[vmem, vmem],
         scratch_shapes=[pltpu.VMEM(shape, F32)] * 4
         + [
-            pltpu.VMEM((2, OWNERS, CAP, S, S), F32),
-            pltpu.VMEM((2, OWNERS, CAP, S, S), F32),
-            pltpu.VMEM((OWNERS, CAP, S), F32),
+            pltpu.VMEM((2, 2, 8, 4, CAP, PART, S), F32),
+            pltpu.VMEM((2, 2, 8, 4, CAP, PART, S), F32),
+            pltpu.VMEM((2, 8, 8, S), F32),
+            pltpu.VMEM((2, 8, 8, S), F32),
+            pltpu.VMEM((2, 2, 4, BLOCKS, PART, S), F32),
+            pltpu.VMEM((2, 2, 2, BLOCKS // 2, PART, S), F32),
+            pltpu.VMEM((2, 2, 2, BLOCKS, PART, S), F32),
             pltpu.VMEM((2, BLOCKS, S, S), F32),
             pltpu.VMEM((TALL, WIDE), F32),
             pltpu.VMEM((TALL, WIDE), BF16),
@@ -415,10 +509,12 @@
             pltpu.VMEM((2, 2, 4, 2, S, S), F32),
             pltpu.VMEM((2, 2, 4, 2, S, S), F32),
             dma((4,)),
-            dma((OWNERS,)),
-            dma((OWNERS,)),
-            dma((2, OWNERS)),
-            dma((2, OWNERS)),
+            dma((2, 8)),
+            dma((2, 8)),
+            dma((2, 2, 8)),
+            dma((2, 2, 8)),
+            dma((2, 2, 6)),
+            dma((2, 2, 6)),
             dma((2, 2, 4, 2)),
             dma((2, 2, 4, 2)),
             dma((2,)),
@@ -429,9 +525,9 @@
         ),
         name="coadd",
     )(
-        table[:3].reshape(3 * SLOTS), coeffs.reshape(4),
+        first, last, piece_slot.reshape(PIECES), piece_extent.reshape(PIECES, 2).T, coeffs.reshape(4),
         piece_flux.reshape(shape), piece_ivar.reshape(shape), warp_rows.reshape(shape), warp_cols.reshape(shape),
-        ids, basis, *[jnp.asarray(t) for t in tables],
+        basis, *[jnp.asarray(t) for t in tables],
     )
     return coadd, weight
 

time: 156 us -> 130 us (0.83)
  Pallas kernels: 148 us -> 124 us
  local copies, waits for them, and re-layouts: 5.35 us -> 3.14 us
    pallas_call x1, Pallas kernels: 148 us -> 124 us  [on_device(): pl.pallas_call(kernel, out_shape=[jax.ShapeDtypeStruct((BR * S, S), F32)]...]
where the time goes in v1:
time: 130 us; the launch traced here: 129 us
  Pallas kernels  124 us (95%)
  local copies, waits for them, and re-layouts  3.14 us (2%)
    pallas_call x1, Pallas kernels, on_device(): pl.pallas_call(kernel, out_shape=[jax.ShapeDtypeStruct((BR * S, S), F32)]...  124 us
    unnamed x2, local copies, waits for them, and re-layouts  3.14 us

profile of v1, /device:TPU:24, one launch (start us, length us, event | category | flops | bytes accessed | tf_op | source)
XLA Modules:
  0.0 128.7 jit_solution(1756341991224727396)
XLA Ops:
  0.6 1.3 select_reduce_fusion
  1.9 123.7 %coadd.1 = (f32[256,128]{1,0:T(8,128)}, f32[256,128]{1,0:T(8,128)}) custom-call(s32[32]{0:T(128)} %get-tuple-element.3.first_ref, s32[32]{0:T(128)} %get-tuple-element.2.last_ref, s32[32]{0:T(128)} %bitcast.15, s32[2,32]{1,0:T(2,128)} %bitcast.14, f32[4]{0:T(128)} %bitcast.16, f32[32,128,128]{2,1,0:T(8,128)} %bitcast.10, f32[32,128,128]{2,1,0:T(8,128)} %bitcast.11, ...), custom_call_target="tpu_custom_call" | custom-call | tf_op jit(solution)/shard_map/coadd/pallas_call | solution.py:487
  125.6 1.6 %copy.25 = f32[256,128]{1,0:T(8,128)} copy(f32[256,128]{1,0:T(8,128)} %get-tuple-element.6) | data formatting | bytes 262144
  127.1 1.6 %copy.26 = f32[256,128]{1,0:T(8,128)} copy(f32[256,128]{1,0:T(8,128)} %get-tuple-element.7) | data formatting | bytes 262144

commit v2 on v1

--- a/solution.py
+++ b/solution.py
@@ -25,6 +25,8 @@
 WIDE = (BC + 1) * S
 TALL = BR * S + 2 * HALO
 STRIDE = 11
+TABLES = 15
+THIRD = WIDE // 3
 
 
 def split_np(table):
@@ -41,11 +43,15 @@
     full = np.concatenate([np.cos(freq[:, None] * places), np.sin(freq[:, None] * places)])
     kern = np.concatenate([np.cos(freq[:, None] * taps), np.sin(freq[:, None] * taps)])
     mid = full[:, HALO : HALO + S] / (LEN // 2)
-    return [
+    parts = [
         part
         for table in (full, full.T, mid, mid.T, kern, kern.T)
         for part in split_np(np.ascontiguousarray(table))
     ]
+    high, low = parts[:2]
+    for cut in (slice(0, HALO), slice(LEN - HALO, LEN)):
+        parts.append(np.concatenate([high[:, cut], high[:, cut], low[:, cut]], axis=1))
+    return parts
 
 
 def split(x):
@@ -65,15 +71,20 @@
 
 
 def kernel(
-    first_ref, last_ref, slot_ref, extent_ref, coef_ref, flux_hbm, ivar_hbm, rows_hbm, cols_hbm, basis_ref,
-    full_h, full_l, fullt_h, fullt_l, mid_h, mid_l, midt_h, midt_l,
-    kern_h, kern_l, kernt_h, kernt_l,
-    coadd_ref, weight_ref,
+    first_ref, last_ref, slot_ref, extent_ref, coef_ref, flux_hbm, ivar_hbm, rows_hbm, cols_hbm, *rest,
+):
+    tables_hbm, (coadd_ref, weight_ref) = rest[:TABLES], rest[TABLES : TABLES + 2]
+    tables_v, scratch = rest[TABLES + 2 : 2 * TABLES + 2], rest[2 * TABLES + 2 :]
+    (
+        basis_ref, full_h, full_l, fullt_h, fullt_l, mid_h, mid_l, midt_h, midt_l,
+        kern_h, kern_l, kernt_h, kernt_l, edge_first, edge_last,
+    ) = tables_v
+    (
     flux_v, ivar_v, rows_v, cols_v, send, recv, ids_own, ids_recv, dense, passed, arrived, canvas, image,
     vh, vl, fxh, fxl, spec, numer, own_out, land,
     in_sem, ids_send_sem, ids_recv_sem, send_sem, recv_sem, pass_send, pass_recv,
-    chain_send, chain_recv, halo_send, halo_recv,
-):
+    chain_send, chain_recv, halo_send, halo_recv, table_sem, own_rows, edges,
+    ) = scratch
     v = lax.axis_index("visit")
     b = lax.axis_index("bulk")
     x, y, c = b // 8, (b // 2) % 4, b % 2
@@ -83,11 +94,14 @@
 
     right, left = (v + 1) % VISITS, (v + VISITS - 1) % VISITS
 
+    pairs = ((flux_hbm, flux_v), (ivar_hbm, ivar_v), (rows_hbm, rows_v), (cols_hbm, cols_v))
     loads = [
-        pltpu.make_async_copy(src, dst, in_sem.at[k])
-        for k, (src, dst) in enumerate(
-            ((flux_hbm, flux_v), (ivar_hbm, ivar_v), (rows_hbm, rows_v), (cols_hbm, cols_v))
-        )
+        pltpu.make_async_copy(src.at[q * 8 : q * 8 + 8], dst.at[q * 8 : q * 8 + 8], in_sem.at[4 * k + q])
+        for k, (src, dst) in enumerate(pairs)
+        for q in range(4)
+    ]
+    table_loads = [
+        pltpu.make_async_copy(src, dst, table_sem.at[k]) for k, (src, dst) in enumerate(zip(tables_hbm, tables_v))
     ]
     for load in loads:
         load.start()
@@ -134,6 +148,8 @@
 
     for load in loads:
         load.wait()
+    for load in table_loads:
+        load.start()
     pl.semaphore_wait(barrier, OWNERS - 1 + 2)
 
     def id_copy(route, j):
@@ -204,6 +220,8 @@
     for r in range(CAP):
         warp_slot(0, r)
 
+    for load in table_loads:
+        load.wait()
     taps = coef_ref[0] * basis_ref[0]
     for k in range(1, 4):
         taps = taps + coef_ref[k] * basis_ref[k]
@@ -308,53 +326,57 @@
     def chunk_of(direction, step):
         return (v + 4 - step) % VISITS if direction == 0 else (v + 4 + step) % VISITS
 
-    def chain_copy(what, direction, step, half):
+    def chain_copy(what, direction, step, quarter):
         return pltpu.make_async_remote_copy(
-            src_ref=own_out.at[what, direction, step, half], dst_ref=land.at[what, direction, step, half],
-            send_sem=chain_send.at[what, direction, step, half],
-            recv_sem=chain_recv.at[what, direction, step, half],
+            src_ref=own_out.at[what, direction, step, quarter], dst_ref=land.at[what, direction, step, quarter],
+            send_sem=chain_send.at[what, direction, step, quarter],
+            recv_sem=chain_recv.at[what, direction, step, quarter],
             device_id=(right if direction == 0 else left, b), device_id_type=MESH)
 
     def chain_first(what, own):
-        for direction in (0, 1):
-            own_out[what, direction, 0, direction] = own(direction, chunk_of(direction, 0))
-            chain_copy(what, direction, 0, direction).start()
-
-    def chain_step(what, step, own):
         for near in (0, 1):
             for direction in (0, 1):
-                half = direction if near == 0 else 1 - direction
-                value = own(half, chunk_of(direction, step))
-                if step > 1 or half == direction:
-                    chain_copy(what, direction, step - 1, half).wait_recv()
-                    value = value + land[what, direction, step - 1, half]
-                own_out[what, direction, step, half] = value
-                chain_copy(what, direction, step, half).start()
-
-    def chain_last(what, half, own):
+                quarter = 2 * direction + near
+                own_out[what, direction, 0, quarter] = own(quarter, chunk_of(direction, 0))
+                chain_copy(what, direction, 0, quarter).start()
+
+    def chain_step(what, step, own):
+        for near in range(4):
+            for direction in (0, 1):
+                quarter = (2 * direction + near) % 4
+                value = own(quarter, chunk_of(direction, step))
+                if step > 1 or near < 2:
+                    chain_copy(what, direction, step - 1, quarter).wait_recv()
+                    value = value + land[what, direction, step - 1, quarter]
+                own_out[what, direction, step, quarter] = value
+                chain_copy(what, direction, step, quarter).start()
+
+    def chain_last(what, quarter, own):
         for direction in (0, 1):
-            chain_copy(what, direction, 3, half).wait_recv()
-        return own(half, v) + (land[what, 0, 3, half] + land[what, 1, 3, half])
-
-    def ivar_own(half, chunk):
-        return canvas[1, half * BC + chunk]
+            chain_copy(what, direction, 3, quarter).wait_recv()
+        return own(quarter, v) + (land[what, 0, 3, quarter] + land[what, 1, 3, quarter])
+
+    def ivar_own(quarter, chunk):
+        return canvas[1, quarter // 2 * BC + chunk, quarter % 2 * PART : quarter % 2 * PART + PART, :]
 
     chain_first(1, ivar_own)
     pass_merged(0)
-    for step in (1, 2, 3):
+    for step in (1, 2):
         chain_step(1, step, ivar_own)
     pass_last(0)
 
-    for br in range(BR):
-        before = jnp.zeros((S, HALO), F32)
+    def make_image(br, start):
+        rows = slice(start, start + PART)
+        there = HALO + br * S + start
+        before = jnp.zeros((PART, HALO), F32)
         for j in range(BC + 1):
             if j < BC:
-                cur = canvas[0, br * BC + j] / jnp.maximum(canvas[1, br * BC + j], 1.0)
+                cur = canvas[0, br * BC + j, rows, :] / jnp.maximum(canvas[1, br * BC + j, rows, :], 1.0)
                 piece = jnp.concatenate([before, cur[:, :HALO]], axis=1)
                 before = cur[:, HALO:]
             else:
-                piece = jnp.concatenate([before, jnp.zeros((S, HALO), F32)], axis=1)
-            image[HALO + br * S : HALO + br * S + S, j * S : j * S + S] = piece
+                piece = jnp.concatenate([before, jnp.zeros((PART, HALO), F32)], axis=1)
+            image[there : there + PART, j * S : j * S + S] = piece
 
     def halo_copy(side):
         start, to = (BR * S, 0) if side == 0 else (HALO, HALO + BR * S)
@@ -366,41 +388,58 @@
 
     has_next, has_before = b < OWNERS - 1, b > 0
 
+    make_image(1, PART)
+
     @pl.when(has_next)
     def _():
         halo_copy(0).start()
 
+    make_image(0, 0)
+
     @pl.when(has_before)
     def _():
         halo_copy(1).start()
 
+    make_image(0, PART)
+    make_image(1, 0)
     mine = slice(HALO, HALO + BR * S)
     vh[mine, :], vl[mine, :] = split(image[mine, :])
-    for half in range(BR):
-        weight_ref[half * S : half * S + S, :] = chain_last(1, half, ivar_own)
-
-    @pl.when(has_before)
-    def _():
-        halo_copy(0).wait_recv()
-
-    @pl.when(has_next)
-    def _():
-        halo_copy(1).wait_recv()
-
     for top in (0, HALO + BR * S):
-        edge = slice(top, top + HALO)
-        vh[edge, :], vl[edge, :] = split(image[edge, :])
-
-    def row_stage(j, carry):
-        at = pl.ds(pl.multiple_of(j * S, S), S)
+        vh[top : top + HALO, :] = jnp.zeros((HALO, WIDE), BF16)
+        vl[top : top + HALO, :] = jnp.zeros((HALO, WIDE), BF16)
+    chain_step(1, 3, ivar_own)
+
+    def own_stage(j, carry):
+        at = pl.ds(pl.multiple_of(j * THIRD, S), THIRD)
         for rt in range(BR):
             here = slice(rt * S, rt * S + LEN)
-            out = dot3((full_h[...], full_l[...]), (vh[here, at], vl[here, at]))
+            own_rows[rt * LEN : rt * LEN + LEN, at] = dot3((full_h[...], full_l[...]), (vh[here, at], vl[here, at]))
+        return carry
+
+    lax.fori_loop(0, 3, own_stage, 0)
+
+    @pl.when(has_before)
+    def _():
+        halo_copy(0).wait_recv()
+
+    @pl.when(has_next)
+    def _():
+        halo_copy(1).wait_recv()
+
+    for rt, top in enumerate((0, HALO + BR * S)):
+        high, low = split(image[top : top + HALO, :])
+        for k, part in enumerate((high, low, high)):
+            edges[rt, k * HALO : k * HALO + HALO, :] = part
+
+    def edge_stage(j, carry):
+        at = pl.ds(pl.multiple_of(j * THIRD, S), THIRD)
+        for rt, table in enumerate((edge_first, edge_last)):
             there = slice(rt * LEN, rt * LEN + LEN)
+            out = own_rows[there, at] + jnp.dot(table[...], edges[rt, :, at], preferred_element_type=F32)
             fxh[there, at], fxl[there, at] = split(out)
         return carry
 
-    lax.fori_loop(0, BC + 1, row_stage, 0)
+    lax.fori_loop(0, 3, edge_stage, 0)
 
     def tile(bc):
         at = pl.ds(pl.multiple_of(bc * S, S), LEN)
@@ -421,8 +460,8 @@
             matched = dot3((midt_h[...], midt_l[...]), split(back))
             numer[rt, bc] = canvas[1, rt * BC + bc] * matched
 
-    def numer_own(half, chunk):
-        return numer[half, chunk]
+    def numer_own(quarter, chunk):
+        return numer[quarter // 2, chunk, quarter % 2 * PART : quarter % 2 * PART + PART, :]
 
     def tile_step(k, carry):
         near = (k + 1) // 2
@@ -440,9 +479,10 @@
         return carry
 
     lax.fori_loop(0, VISITS, tile_step, 0)
-    for half in range(BR):
-        at = slice(half * S, half * S + S)
-        coadd_ref[at, :] = chain_last(0, half, numer_own) / jnp.maximum(weight_ref[at, :], 1.0)
+    for quarter in range(4):
+        weight_ref[quarter * PART : quarter * PART + PART, :] = chain_last(1, quarter, ivar_own)
+    for quarter in range(4):
+        coadd_ref[quarter * PART : quarter * PART + PART, :] = chain_last(0, quarter, numer_own)
 
     def drain(n, carry):
         route, j = n % 2, n // 2
@@ -458,10 +498,10 @@
                 pass_copy(plane, route, m).wait_send()
     for what in (0, 1):
         for direction in (0, 1):
-            chain_copy(what, direction, 0, direction).wait_send()
-            for step in (1, 2, 3):
-                for half in (0, 1):
-                    chain_copy(what, direction, step, half).wait_send()
+            for step in (0, 1, 2, 3):
+                for quarter in range(4):
+                    if step > 0 or quarter // 2 == direction:
+                        chain_copy(what, direction, step, quarter).wait_send()
 
     @pl.when(has_next)
     def _():
@@ -484,12 +524,14 @@
     hbm = pl.BlockSpec(memory_space=pl.ANY)
     tables = dft_tables()
     dma = pltpu.SemaphoreType.DMA
-    coadd, weight = pl.pallas_call(
+    numerator, weight = pl.pallas_call(
         kernel,
         out_shape=[jax.ShapeDtypeStruct((BR * S, S), F32)] * 2,
-        in_specs=[smem] * 5 + [hbm] * 4 + [vmem] * (1 + len(tables)),
+        in_specs=[smem] * 5 + [hbm] * (4 + TABLES),
         out_specs=[vmem, vmem],
-        scratch_shapes=[pltpu.VMEM(shape, F32)] * 4
+        scratch_shapes=[pltpu.VMEM(basis.shape, F32)]
+        + [pltpu.VMEM(t.shape, BF16) for t in tables]
+        + [pltpu.VMEM(shape, F32)] * 4
         + [
             pltpu.VMEM((2, 2, 8, 4, CAP, PART, S), F32),
             pltpu.VMEM((2, 2, 8, 4, CAP, PART, S), F32),
@@ -506,19 +548,22 @@
             pltpu.VMEM((BR * LEN, WIDE), BF16),
             pltpu.VMEM((LEN, LEN), F32),
             pltpu.VMEM((BR, BC, S, S), F32),
-            pltpu.VMEM((2, 2, 4, 2, S, S), F32),
-            pltpu.VMEM((2, 2, 4, 2, S, S), F32),
-            dma((4,)),
+            pltpu.VMEM((2, 2, 4, 4, PART, S), F32),
+            pltpu.VMEM((2, 2, 4, 4, PART, S), F32),
+            dma((16,)),
             dma((2, 8)),
             dma((2, 8)),
             dma((2, 2, 8)),
             dma((2, 2, 8)),
             dma((2, 2, 6)),
             dma((2, 2, 6)),
-            dma((2, 2, 4, 2)),
-            dma((2, 2, 4, 2)),
+            dma((2, 2, 4, 4)),
+            dma((2, 2, 4, 4)),
             dma((2,)),
             dma((2,)),
+            dma((TABLES,)),
+            pltpu.VMEM((BR * LEN, WIDE), F32),
+            pltpu.VMEM((BR, 3 * HALO, WIDE), BF16),
         ],
         compiler_params=pltpu.CompilerParams(
             collective_id=0, has_side_effects=True, vmem_limit_bytes=60 * 1024 * 1024
@@ -529,7 +574,7 @@
         piece_flux.reshape(shape), piece_ivar.reshape(shape), warp_rows.reshape(shape), warp_cols.reshape(shape),
         basis, *[jnp.asarray(t) for t in tables],
     )
-    return coadd, weight
+    return numerator / jnp.maximum(weight, 1.0), jnp.maximum(weight, 0.0)
 
 
 def solution(mesh):

time: 130 us -> 126 us (0.969)
  local copies, waits for them, and re-layouts: 3.14 us -> 0 us
  Pallas kernels: 124 us -> 121 us
  other arithmetic: 1.26 us -> 2.94 us
    unnamed x2 -> x0, local copies, waits for them, and re-layouts: 3.14 us -> none
    pallas_call x1, Pallas kernels: 124 us -> 121 us  [on_device(): pl.pallas_call(kernel, out_shape=[jax.ShapeDtypeStruct((BR * S, S), F32)]...]
    max x0 -> x1, other arithmetic: none -> 1.68 us  [on_device(): return (numerator / jnp.maximum(weight, 1.0), jnp.maximum(weight, 0.0))]
where the time goes in v2:
time: 126 us; the launch traced here: 125 us
  Pallas kernels  121 us (96%)
  other arithmetic  2.94 us (2%)
    pallas_call x1, Pallas kernels, on_device(): pl.pallas_call(kernel, out_shape=[jax.ShapeDtypeStruct((BR * S, S), F32)]...  121 us

profile of v2, /device:TPU:24, one launch (start us, length us, event | category | flops | bytes accessed | tf_op | source)
XLA Modules:
  0.0 124.5 jit_solution(5051086356282703363)
XLA Ops:
  0.6 1.3 %select_reduce_fusion = (s32[32]{0:T(128)}, s32[32]{0:T(128)}) fusion(s32[32]{0:T(128)} %bitcast.17), kind=kLoop, calls=%fused_computation.2 | loop fusion | flops 5056 | bytes 384 | tf_op jit(solution)/shard_map/reduce_max | solution.py:520
  1.9 121.0 %coadd.1 = (f32[256,128]{1,0:T(8,128)}, f32[256,128]{1,0:T(8,128)}) custom-call(s32[32]{0:T(128)} %get-tuple-element.7.first_ref, s32[32]{0:T(128)} %get-tuple-element.6.last_ref, s32[32]{0:T(128)} %bitcast.15, s32[2,32]{1,0:T(2,128)} %bitcast.14, f32[4]{0:T(128)} %bitcast.16, f32[32,128,128]{2,1,0:T(8,128)} %bitcast.10, f32[32,128,128]{2,1,0:T(8,128)} %bitcast.11, ...), custom_call_target="tpu_custom_call" | custom-call | tf_op jit(solution)/shard_map/coadd/pallas_call | solution.py:527
  122.9 1.7 %broadcast_maximum_fusion = (f32[256,128]{1,0:T(8,128)}, f32[256,128]{1,0:T(8,128)}) fusion(f32[256,128]{1,0:T(8,128)} %get-tuple-element.5, f32[256,128]{1,0:T(8,128)} %get-tuple-element.4), kind=kLoop, calls=%fused_computation.1 | loop fusion | flops 98304 | bytes 524288 | tf_op jit(solution)/shard_map/max | solution.py:577
